TPU v7x, 256 devices: a whole 4x4x8 slice. The times are simulated.
256 devices in a mesh: dp: 32 (over z, x_hi, core), expert: 8 (over x_lo, y).
Axes of the slice: x: 4 (x_hi: 2, x_lo: 2; x = x_hi * 2 + x_lo), y: 4, z: 8, core: 2. Of those that a mesh axis runs over, the one named last changes fastest.
Arguments:
- x_rows: bfloat16 [131072, 1024], P(('dp', 'expert')), may hold values from -24 to 24
- dy_rows: bfloat16 [131072, 2048], P(('dp', 'expert')), may hold values from -0.0234375 to 0.0234375
- seg_blocks: int32 [256, 8], replicated, may hold values from 0 to 2, as said below
Outputs:
- expert_grad: float32 [8, 1024, 2048], P(None, 'dp', 'expert')
Inputs may be any that keep to these rules, and one draw needn't show every extreme that they name: `seg_blocks`: on every device the entries sum to at most 4; one expert has exactly 2 blocks on every device.
All inputs are finite; a program needn't handle non-finite values.
Results may differ from a plain program's by a relative error of at most 0.0003.
Values may be sent and summed in bfloat16 or wider, within the bound.
A program may use at most 128 MiB of HBM per device.

v0:
```python
import jax
import jax.numpy as jnp
from jax import lax
from jax.sharding import PartitionSpec as P

BLOCK = 128
CAP = 2


def contract(left, right):
    return lax.dot_general(
        left, right, (((0,), (0,)), ((), ())), preferred_element_type=jnp.float32
    )


def shards(x_rows, dy_rows, seg_blocks):
    rows, hid = x_rows.shape
    ffn = dy_rows.shape[1]
    n_exp = lax.axis_size("expert")
    n_dp = lax.axis_size("dp")
    experts = seg_blocks.shape[1]
    nblk = rows // BLOCK
    device = lax.axis_index(("dp", "expert"))
    counts = lax.dynamic_slice(seg_blocks, (device, 0), (1, experts))[0]
    starts = jnp.cumsum(counts) - counts
    slots = jnp.arange(CAP, dtype=jnp.int32)
    live = slots[None, :] < counts[:, None]
    index = jnp.where(live, starts[:, None] + slots[None, :], 0).reshape(-1)
    keep = live.reshape(-1)[:, None, None]
    xsend = jnp.where(keep, x_rows.reshape(nblk, BLOCK, hid)[index], jnp.zeros((), x_rows.dtype))
    dysend = jnp.where(keep, dy_rows.reshape(nblk, BLOCK, ffn)[index], jnp.zeros((), dy_rows.dtype))
    xsend = xsend.reshape(experts, CAP * BLOCK, hid)
    dysend = dysend.reshape(experts, CAP * BLOCK, ffn)
    got_x, got_dy = (
        lax.all_to_all(xsend, "expert", split_axis=0, concat_axis=0, tiled=True),
        lax.all_to_all(dysend, "expert", split_axis=0, concat_axis=0, tiled=True),
    )
    got_x = got_x.reshape(n_exp * CAP * BLOCK, hid)
    got_dy = got_dy.reshape(n_exp * CAP * BLOCK, ffn)
    summed = lax.psum_scatter(contract(got_x, got_dy), "dp", scatter_dimension=0, tiled=True)
    return lax.all_to_all(
        summed.reshape(1, hid // n_dp, ffn), "expert", split_axis=2, concat_axis=0, tiled=True
    )


def solution(mesh):
    in_specs = (P(("dp", "expert"), None), P(("dp", "expert"), None), P())
    out_specs = P(None, "dp", "expert")
    return jax.shard_map(shards, mesh=mesh, in_specs=in_specs, out_specs=out_specs, check_vma=False)
```

profile of v0, /device:TPU:2, one launch (start us, length us, event | category | flops | bytes accessed | tf_op | source)
XLA Modules:
  0.0 380.6 jit_solution(2443288582051426192)
XLA Ops:
  6.5 0.0 copy-start
  6.5 1.0 dynamic-slice_reduce_fusion
  7.6 0.1 iota_compare_fusion
  7.6 0.2 reduce-window.8
  7.8 0.1 add_select_fusion
  7.9 0.1 select_n.41
  8.0 0.1 copy.9
  8.1 0.1 broadcast_bitcast_fusion
  8.2 4.0 %gather_fusion = bf16[16,128,1024]{2,1,0:T(8,128)(2,1)} fusion(bf16[4,128,1024]{2,1,0:T(8,128)(2,1)} %bitcast.27, s32[1024]{0:T(1024)S(1)} %pad_clamp_fusion), kind=kCustom, calls=%fused_computation | custom fusion | bytes 8388672 | tf_op jit(solution)/shard_map/gather | solution.py:30
  12.1 6.5 %copy.10 = bf16[8,256,1024]{1,2,0:T(8,128)(2,1)} copy(bf16[8,256,1024]{2,1,0:T(8,128)(2,1)} %bitcast.26) | data formatting | bytes 8388608 | tf_op jit(solution)/shard_map/gather | solution.py:30
  18.6 4.4 %broadcast_select_fusion = bf16[8,256,1024]{1,2,0:T(8,128)(2,1)} fusion(bf16[8,256,1024]{1,2,0:T(8,128)(2,1)} %copy.10, pred[8,256]{1,0:T(8,128)(4,1)S(1)} %broadcast_bitcast_fusion), kind=kLoop, calls=%fused_computation.4 | loop fusion | flops 2097152 | bytes 8390656 | tf_op jit(solution)/shard_map/jit(_where)/select_n | solution.py:30
  23.0 6.7 %all-to-all-start = ((bf16[8,256,1024]{1,2,0:T(8,128)(2,1)}), bf16[8,256,1024]{1,2,0:T(8,128)(2,1)}, u32[]{:S(2)}, u32[]{:S(2)}) async-start(bf16[8,256,1024]{1,2,0:T(8,128)(2,1)} %broadcast_select_fusion), calls=%async_computation | async-start | bytes 8388608 | tf_op jit(solution)/shard_map/all_to_all | solution.py:35
  29.7 0.0 reduce-scatter.2.cloned.1.call-start
  29.7 0.0 copy-done
  29.7 4.6 %gather_fusion.1 = bf16[16,128,2048]{2,1,0:T(8,128)(2,1)} fusion(bf16[4,128,2048]{2,1,0:T(8,128)(2,1)S(1)} %bitcast.24, s32[1024]{0:T(1024)S(1)} %pad_clamp_fusion), kind=kCustom, calls=%fused_computation.1 | custom fusion | bytes 16777280 | tf_op jit(solution)/shard_map/gather | solution.py:31
  34.3 7.3 %bitcast_select_fusion = bf16[8,256,2048]{2,1,0:T(8,128)(2,1)} fusion(pred[8,256]{1,0:T(8,128)(4,1)S(1)} %broadcast_bitcast_fusion, bf16[8,256,2048]{2,1,0:T(8,128)(2,1)} %bitcast.25), kind=kLoop, calls=%fused_computation.2 | loop fusion | flops 4194304 | bytes 16779264 | tf_op jit(solution)/shard_map/jit(_where)/select_n | solution.py:31
  41.6 35.5 %all-to-all-done = bf16[8,256,1024]{1,2,0:T(8,128)(2,1)} async-done(((bf16[8,256,1024]{1,2,0:T(8,128)(2,1)}), bf16[8,256,1024]{1,2,0:T(8,128)(2,1)}, u32[]{:S(2)}, u32[]{:S(2)}) %all-to-all-start) | async-done | bytes 4194336 | tf_op jit(solution)/shard_map/all_to_all | solution.py:35
  77.0 98.7 %all_to_all.28 = bf16[8,256,2048]{2,1,0:T(8,128)(2,1)S(1)} all-to-all(bf16[8,256,2048]{2,1,0:T(8,128)(2,1)} %bitcast_select_fusion), channel_id=1, replica_groups=mesh['dp'=32,'expert'=8] {'expert'}, dimensions={0} | all-to-all | bytes 16777216 | tf_op jit(solution)/shard_map/all_to_all | solution.py:36
  175.7 12.7 %convolution_bitcast_fusion = f32[1024,2048]{1,0:T(8,128)} fusion(bf16[8,256,1024]{1,2,0:T(8,128)(2,1)} %all-to-all-done, bf16[8,256,2048]{2,1,0:T(8,128)(2,1)S(1)} %all_to_all.28), kind=kOutput, calls=%fused_computation.3 | convolution fusion | flops 8589934592 | bytes 20971520 | tf_op jit(solution)/shard_map/dot_general | solution.py:11
  188.5 0.0 reduce-scatter.2.cloned.1.call-update
  188.5 155.2 %reduce-scatter.2.cloned.1.call-done = f32[32,2048]{1,0:T(8,128)} async-done(((f32[1024,2048]{1,0:T(8,128)}), f32[32,2048]{1,0:T(8,128)}) %reduce-scatter.2.cloned.1.call-update) | async-done | bytes 262160 | tf_op jit(solution)/shard_map/reduce_scatter | solution.py:40
  343.7 2.1 copy.11
  345.8 0.5 broadcast.54
  346.3 10.3 %reduce.3 = f32[2048,32]{1,0:T(8,128)} reduce(f32[2048,1,32]{2,1,0:T(1,128)S(1)} %bitcast.28, f32[]{:T(128)} %broadcast.54), dimensions={1}, to_apply=%bitcast.19.reduce_sub_computation | reduce | bytes 524292
  356.7 1.7 reshape.143
  358.3 11.3 %all_to_all.29 = f32[8,1,8192]{2,1,0:T(1,128)S(1)} all-to-all(f32[8,1,8192]{2,1,0:T(1,128)S(1)} %reshape.143), channel_id=1, replica_groups=mesh['dp'=32,'expert'=8] {'expert'}, dimensions={0} | all-to-all | bytes 524288 | tf_op jit(solution)/shard_map/all_to_all | solution.py:41
  369.7 1.3 reduce.4
  370.9 1.8 reshape.144
  372.8 1.0 copy.12
  (3 shorter events, 0.0 us)
Async XLA Ops:
  6.5 23.2 %copy-start = (bf16[512,2048]{1,0:T(8,128)(2,1)S(1)}, bf16[512,2048]{1,0:T(8,128)(2,1)}, u32[]{:S(2)}) copy-start(bf16[512,2048]{1,0:T(8,128)(2,1)} %param.4) | copy-start | bytes 6291460
  23.0 54.0 %all-to-all-start = ((bf16[8,256,1024]{1,2,0:T(8,128)(2,1)}), bf16[8,256,1024]{1,2,0:T(8,128)(2,1)}, u32[]{:S(2)}, u32[]{:S(2)}) async-start(bf16[8,256,1024]{1,2,0:T(8,128)(2,1)} %broadcast_select_fusion), calls=%async_computation | async-start | bytes 8388608 | tf_op jit(solution)/shard_map/all_to_all | solution.py:35
  29.7 314.0 %reduce-scatter.2.cloned.1.call-start = ((), (), s32[]{:S(2)}) async-start(), calls=%async_computation.4 | async-start | bytes 8650752 | tf_op jit(solution)/shard_map/reduce_scatter | solution.py:40
Sparse Core Ops, SparseCore 0:
  188.6 155.0 reduce-scatter.1
where the time goes:
time: 381 us
  waiting for transfers between devices  191 us (50%)
  blocking collectives  110 us (29%)
  other arithmetic  23.6 us (6%)
  local copies, waits for them, and re-layouts  23.4 us (6%)
  between operations  13.4 us (4%)
  matrix products  12.7 us (3%)
  starting transfers between devices  6.68 us (2%)
    reduce_scatter x1, waiting for transfers between devices, shards(): lax.psum_scatter(contract(got_x, got_dy), 'dp', scatter_dimension=0, tile...  155 us
    all_to_all x1, blocking collectives, shards(): lax.all_to_all(dysend, 'expert', split_axis=0, concat_axis=0, tiled=True)  98.7 us
    all_to_all x1, waiting for transfers between devices, shards(): lax.all_to_all(xsend, 'expert', split_axis=0, concat_axis=0, tiled=True)  35.5 us
    dot_general x1, matrix products, contract(): lax.dot_general(left, right, (((0,), (0,)), ((), ())), preferred_element_...  12.7 us
    all_to_all x1, blocking collectives, shards(): lax.all_to_all(summed.reshape(1, hid // n_dp, ffn), 'expert', split_axis=...  11.3 us
    gather x2, local copies, waits for them, and re-layouts, shards(): x_rows.reshape(nblk, BLOCK, hid)[index]  10.4 us
    unnamed x1, other arithmetic  10.3 us
  transfers between devices with their start and end apart: 2, of which 2 were waited for; matrix products, arithmetic and copies ran while one was open for 3% of the time, Pallas kernels for 0%

commit v1 on v0

--- a/solution.py
+++ b/solution.py
@@ -38,8 +38,16 @@
     got_x = got_x.reshape(n_exp * CAP * BLOCK, hid)
     got_dy = got_dy.reshape(n_exp * CAP * BLOCK, ffn)
     summed = lax.psum_scatter(contract(got_x, got_dy), "dp", scatter_dimension=0, tiled=True)
-    return lax.all_to_all(
-        summed.reshape(1, hid // n_dp, ffn), "expert", split_axis=2, concat_axis=0, tiled=True
+    return jnp.concatenate(
+        lax.all_to_all(
+            jnp.stack(
+                jnp.split(summed.reshape(1, hid // n_dp, ffn), lax.axis_size("expert"), axis=2)
+            ),
+            "expert",
+            0,
+            0,
+        ),
+        axis=0,
     )
 
 

time: 381 us -> 370 us (0.971)
  other arithmetic: 23.6 us -> 12.1 us
    unnamed x1 -> x0, other arithmetic: 10.3 us -> none
where the time goes in v1:
time: 370 us; the launch traced here: 369 us
  waiting for transfers between devices  191 us (52%)
  blocking collectives  110 us (30%)
  local copies, waits for them, and re-layouts  23.1 us (6%)
  between operations  13.4 us (4%)
  matrix products  12.7 us (3%)
  other arithmetic  12.1 us (3%)
  starting transfers between devices  6.68 us (2%)
    reduce_scatter x1, waiting for transfers between devices, shards(): lax.psum_scatter(contract(got_x, got_dy), 'dp', scatter_dimension=0, tile...  155 us
    all_to_all x1, blocking collectives, shards(): lax.all_to_all(dysend, 'expert', split_axis=0, concat_axis=0, tiled=True)  98.7 us
    all_to_all x1, waiting for transfers between devices, shards(): lax.all_to_all(xsend, 'expert', split_axis=0, concat_axis=0, tiled=True)  35.5 us
    dot_general x1, matrix products, contract(): lax.dot_general(left, right, (((0,), (0,)), ((), ())), preferred_element_...  12.7 us
    all_to_all x1, blocking collectives, shards(): lax.all_to_all(jnp.stack(jnp.split(summed.reshape(1, hid // n_dp, ffn), l...  11.3 us
    gather x2, local copies, waits for them, and re-layouts, shards(): x_rows.reshape(nblk, BLOCK, hid)[index]  10.4 us
  transfers between devices with their start and end apart: 2, of which 2 were waited for; matrix products, arithmetic and copies ran while one was open for 3% of the time, Pallas kernels for 0%

profile of v1, /device:TPU:2, one launch (start us, length us, event | category | flops | bytes accessed | tf_op | source)
XLA Modules:
  0.0 368.7 jit_solution(4740482653055925567)
XLA Ops:
  6.5 0.0 copy-start
  6.5 1.0 dynamic-slice_reduce_fusion
  7.6 0.1 iota_compare_fusion
  7.6 0.2 reduce-window.8
  7.8 0.1 add_select_fusion
  7.9 0.1 select_n.41
  8.0 0.1 copy.5
  8.1 0.1 broadcast_bitcast_fusion
  8.2 4.0 %gather_fusion = bf16[16,128,1024]{2,1,0:T(8,128)(2,1)} fusion(bf16[4,128,1024]{2,1,0:T(8,128)(2,1)} %bitcast.54, s32[1024]{0:T(1024)S(1)} %pad_clamp_fusion), kind=kCustom, calls=%fused_computation | custom fusion | bytes 8388672 | tf_op jit(solution)/shard_map/gather | solution.py:30
  12.1 6.5 %copy.6 = bf16[8,256,1024]{1,2,0:T(8,128)(2,1)} copy(bf16[8,256,1024]{2,1,0:T(8,128)(2,1)} %bitcast.53) | data formatting | bytes 8388608 | tf_op jit(solution)/shard_map/gather | solution.py:30
  18.6 4.4 %broadcast_select_fusion = bf16[8,256,1024]{1,2,0:T(8,128)(2,1)} fusion(bf16[8,256,1024]{1,2,0:T(8,128)(2,1)} %copy.6, pred[8,256]{1,0:T(8,128)(4,1)S(1)} %broadcast_bitcast_fusion), kind=kLoop, calls=%fused_computation.4 | loop fusion | flops 2097152 | bytes 8390656 | tf_op jit(solution)/shard_map/jit(_where)/select_n | solution.py:30
  23.0 6.7 %all-to-all-start = ((bf16[8,256,1024]{1,2,0:T(8,128)(2,1)}), bf16[8,256,1024]{1,2,0:T(8,128)(2,1)}, u32[]{:S(2)}, u32[]{:S(2)}) async-start(bf16[8,256,1024]{1,2,0:T(8,128)(2,1)} %broadcast_select_fusion), calls=%async_computation | async-start | bytes 8388608 | tf_op jit(solution)/shard_map/all_to_all | solution.py:35
  29.7 0.0 reduce-scatter.2.cloned.1.call-start
  29.7 0.0 copy-done
  29.7 4.6 %gather_fusion.1 = bf16[16,128,2048]{2,1,0:T(8,128)(2,1)} fusion(bf16[4,128,2048]{2,1,0:T(8,128)(2,1)S(1)} %bitcast.51, s32[1024]{0:T(1024)S(1)} %pad_clamp_fusion), kind=kCustom, calls=%fused_computation.1 | custom fusion | bytes 16777280 | tf_op jit(solution)/shard_map/gather | solution.py:31
  34.3 7.3 %bitcast_select_fusion = bf16[8,256,2048]{2,1,0:T(8,128)(2,1)} fusion(pred[8,256]{1,0:T(8,128)(4,1)S(1)} %broadcast_bitcast_fusion, bf16[8,256,2048]{2,1,0:T(8,128)(2,1)} %bitcast.52), kind=kLoop, calls=%fused_computation.2 | loop fusion | flops 4194304 | bytes 16779264 | tf_op jit(solution)/shard_map/jit(_where)/select_n | solution.py:31
  41.6 35.5 %all-to-all-done = bf16[8,256,1024]{1,2,0:T(8,128)(2,1)} async-done(((bf16[8,256,1024]{1,2,0:T(8,128)(2,1)}), bf16[8,256,1024]{1,2,0:T(8,128)(2,1)}, u32[]{:S(2)}, u32[]{:S(2)}) %all-to-all-start) | async-done | bytes 4194336 | tf_op jit(solution)/shard_map/all_to_all | solution.py:35
  77.0 98.7 %all_to_all.15 = bf16[8,256,2048]{2,1,0:T(8,128)(2,1)S(1)} all-to-all(bf16[8,256,2048]{2,1,0:T(8,128)(2,1)} %bitcast_select_fusion), channel_id=1, replica_groups=mesh['dp'=32,'expert'=8] {'expert'}, dimensions={0} | all-to-all | bytes 16777216 | tf_op jit(solution)/shard_map/all_to_all | solution.py:36
  175.7 12.7 %convolution_bitcast_fusion = f32[1024,2048]{1,0:T(8,128)} fusion(bf16[8,256,1024]{1,2,0:T(8,128)(2,1)} %all-to-all-done, bf16[8,256,2048]{2,1,0:T(8,128)(2,1)S(1)} %all_to_all.15), kind=kOutput, calls=%fused_computation.3 | convolution fusion | flops 8589934592 | bytes 20971520 | tf_op jit(solution)/shard_map/dot_general | solution.py:11
  188.5 0.0 reduce-scatter.2.cloned.1.call-update
  188.5 155.2 %reduce-scatter.2.cloned.1.call-done = f32[32,2048]{1,0:T(8,128)} async-done(((f32[1024,2048]{1,0:T(8,128)}), f32[32,2048]{1,0:T(8,128)}) %reduce-scatter.2.cloned.1.call-update) | async-done | bytes 262160 | tf_op jit(solution)/shard_map/reduce_scatter | solution.py:40
  343.7 0.8 fusion.7
  344.5 0.8 fusion.6
  345.2 0.8 fusion.5
  346.0 0.8 fusion.4
  346.8 0.8 fusion.3
  347.5 0.8 fusion.2
  348.3 0.8 fusion.1
  349.0 0.8 fusion
  349.8 11.3 %all_to_all.16 = f32[8,1,32,256]{3,2,1,0:T(8,128)S(1)} all-to-all(f32[8,1,32,256]{3,2,1,0:T(8,128)S(1)} %fusion), channel_id=1, replica_groups=mesh['dp'=32,'expert'=8] {'expert'}, dimensions={0} | all-to-all | bytes 524288 | tf_op jit(solution)/shard_map/all_to_all | solution.py:42
  361.1 0.7 copy.15
  (3 shorter events, 0.0 us)
Async XLA Ops:
  6.5 23.2 %copy-start = (bf16[512,2048]{1,0:T(8,128)(2,1)S(1)}, bf16[512,2048]{1,0:T(8,128)(2,1)}, u32[]{:S(2)}) copy-start(bf16[512,2048]{1,0:T(8,128)(2,1)} %param.4) | copy-start | bytes 6291460
  23.0 54.0 %all-to-all-start = ((bf16[8,256,1024]{1,2,0:T(8,128)(2,1)}), bf16[8,256,1024]{1,2,0:T(8,128)(2,1)}, u32[]{:S(2)}, u32[]{:S(2)}) async-start(bf16[8,256,1024]{1,2,0:T(8,128)(2,1)} %broadcast_select_fusion), calls=%async_computation | async-start | bytes 8388608 | tf_op jit(solution)/shard_map/all_to_all | solution.py:35
  29.7 314.0 %reduce-scatter.2.cloned.1.call-start = ((), (), s32[]{:S(2)}) async-start(), calls=%async_computation.4 | async-start | bytes 8650752 | tf_op jit(solution)/shard_map/reduce_scatter | solution.py:40
Sparse Core Ops, SparseCore 0:
  188.6 155.0 reduce-scatter.1
